TPU v7x, 8 devices: a whole 2x2x1 slice. The times are simulated.
8 devices in a mesh: replica: 1 (over z), ep: 8 (over y, x, core).
Axes of the slice: x: 2, y: 2, z: 1, core: 2. Of those that a mesh axis runs over, the one named last changes fastest.
Arguments:
- hidden: bfloat16 [8192, 1536], P(('replica', 'ep'))
- route_one: int32 [8192, 8], P(('replica', 'ep'))
- gate_one: float32 [8192, 8], P(('replica', 'ep'))
- route_two: int32 [8192, 8], P(('replica', 'ep'))
- gate_two: float32 [8192, 8], P(('replica', 'ep'))
- w_gate_one: bfloat16 [64, 1536, 512], P('ep')
- w_up_one: bfloat16 [64, 1536, 512], P('ep')
- w_down_one: bfloat16 [64, 512, 1536], P('ep')
- w_gate_two: bfloat16 [64, 1536, 512], P('ep')
- w_up_two: bfloat16 [64, 1536, 512], P('ep')
- w_down_two: bfloat16 [64, 512, 1536], P('ep')
- old_map: int32 [2, 64], replicated
- new_map: int32 [2, 64], replicated
Outputs:
- output 1: bfloat16 [8192, 1536], P(('replica', 'ep'))
- output 2: bfloat16 [64, 1536, 512], P('ep')
- output 3: bfloat16 [64, 1536, 512], P('ep')
- output 4: bfloat16 [64, 512, 1536], P('ep')
- output 5: bfloat16 [64, 1536, 512], P('ep')
- output 6: bfloat16 [64, 1536, 512], P('ep')
- output 7: bfloat16 [64, 512, 1536], P('ep')
All inputs are finite; a program needn't handle non-finite values.
Results may differ from a plain program's by a relative error of at most 0.00519.
Values are sent between devices in bfloat16 or wider.
A program may use at most 1 GiB of HBM per device.

v0:
```python
import jax
import jax.numpy as jnp
from jax import lax
from jax.sharding import PartitionSpec as P


def expert_ffn(rows_in, w_gate, w_up, w_down):
    gate_act = jnp.einsum('gsqd,sdf->gsqf', rows_in, w_gate, preferred_element_type=jnp.float32)
    up_act = jnp.einsum('gsqd,sdf->gsqf', rows_in, w_up, preferred_element_type=jnp.float32)
    inner = (jax.nn.silu(gate_act) * up_act).astype(jnp.bfloat16)
    return jnp.einsum('gsqf,sfd->gsqd', inner, w_down, preferred_element_type=jnp.float32).astype(jnp.bfloat16)


def route_plan(route, layout, capacity):
    holds = route.reshape(-1)[:, None] == layout[None, :]
    first_hold = (holds & (jnp.cumsum(holds, axis=1) == 1)).astype(jnp.int32)
    order_in = jnp.sum(jnp.cumsum(first_hold, axis=0) * first_hold, axis=1) - 1
    return jnp.argmax(first_hold, axis=1) * capacity + order_in


def moe_layer(hidden, route, gates, w_gate, w_up, w_down, layout, group_size):
    tok_dev, top_count = route.shape
    slot_count = w_gate.shape[0]
    d_model = hidden.shape[1]
    capacity = tok_dev // 2
    position = route_plan(route, layout, capacity)
    choice_token = jnp.arange(tok_dev * top_count, dtype=jnp.int32) // top_count
    row_token = jnp.full((group_size * slot_count * capacity,), tok_dev, jnp.int32).at[position].set(choice_token)
    padded = jnp.concatenate([hidden, jnp.zeros((1, d_model), hidden.dtype)], axis=0)
    send_rows = jnp.take(padded, row_token, axis=0).reshape(group_size, slot_count * capacity, d_model)
    received = lax.all_to_all(send_rows, 'ep', 0, 0, tiled=True)
    expert_out = expert_ffn(received.reshape(group_size, slot_count, capacity, d_model), w_gate, w_up, w_down)
    back_rows = lax.all_to_all(expert_out.reshape(group_size, slot_count * capacity, d_model), 'ep', 0, 0, tiled=True)
    picked = jnp.take(back_rows.reshape(group_size * slot_count * capacity, d_model),
                      position.reshape(tok_dev, top_count), axis=0)
    mixed = jnp.sum(picked.astype(jnp.float32) * gates[:, :, None], axis=1)
    return (hidden.astype(jnp.float32) + mixed).astype(jnp.bfloat16)


def new_layout(weights, incoming, old_row, new_row, group_size):
    slot_count = weights.shape[0]
    device = lax.axis_index('ep')
    from_dev = (device - group_size // 2) % group_size
    old_from = lax.dynamic_slice(old_row, (from_dev * slot_count,), (slot_count,))
    old_mine = lax.dynamic_slice(old_row, (device * slot_count,), (slot_count,))
    new_mine = lax.dynamic_slice(new_row, (device * slot_count,), (slot_count,))
    source = jnp.argmax(new_mine[:, None] == old_from[None, :], axis=1)
    changed = (old_mine != new_mine)[:, None, None]
    return jnp.where(changed, jnp.take(incoming, source, axis=0), weights)


def migrate_layer(w_gate, w_up, w_down, old_row, new_row, group_size):
    pairs = [(src_dev, (src_dev + group_size // 2) % group_size) for src_dev in range(group_size)]
    return tuple(new_layout(weight, lax.ppermute(weight, 'ep', pairs), old_row, new_row, group_size)
                 for weight in (w_gate, w_up, w_down))


def solution(mesh):
    group_size = mesh.shape['ep']
    tok_spec = P(('replica', 'ep'), None)
    slot_spec = P('ep', None, None)
    map_spec = P(None, None)

    def body(hidden, route_one, gate_one, route_two, gate_two, w_gate_one, w_up_one, w_down_one,
             w_gate_two, w_up_two, w_down_two, old_map, new_map):
        gate_one_new, up_one_new, down_one_new = migrate_layer(
            w_gate_one, w_up_one, w_down_one, old_map[0], new_map[0], group_size)
        hidden_mid = moe_layer(hidden, route_one, gate_one, gate_one_new, up_one_new, down_one_new,
                               new_map[0], group_size)
        gate_two_new, up_two_new, down_two_new = migrate_layer(
            w_gate_two, w_up_two, w_down_two, old_map[1], new_map[1], group_size)
        hidden_out = moe_layer(hidden_mid, route_two, gate_two, gate_two_new, up_two_new, down_two_new,
                               new_map[1], group_size)
        return (hidden_out, gate_one_new, up_one_new, down_one_new, gate_two_new, up_two_new, down_two_new)

    in_specs = (tok_spec,) * 5 + (slot_spec,) * 6 + (map_spec, map_spec)
    out_specs = (tok_spec,) + (slot_spec,) * 6
    return jax.shard_map(body, mesh=mesh, in_specs=in_specs, out_specs=out_specs, check_vma=False)
```

profile of v0, /device:TPU:0, one launch (start us, length us, event | category | flops | bytes accessed | tf_op | source)
XLA Modules:
  0.0 7580.0 jit_solution(4371736221677350692)
XLA Ops:
  12.6 34.0 reduce-window.14
  53.4 30.5 scatter_custom_fusion
  86.7 146.0 %gather_fusion.2 = bf16[32768,1536]{1,0:T(8,128)(2,1)} fusion(bf16[1025,1536]{1,0:T(8,128)(2,1)S(1)} %concatenate.6, s32[32768]{0:T(1024)S(1)} %fusion.42), kind=kCustom, calls=%fused_computation.2.clone | custom fusion | bytes 201457664 | tf_op jit(solution)/shard_map/jit(_take)/gather | solution.py:30
  232.7 65.0 broadcast_select_fusion.1
  316.0 1345.7 %collective-permute-done.1 = bf16[8,1536,512]{2,1,0:T(8,128)(2,1)} collective-permute-done((bf16[8,1536,512]{2,1,0:T(8,128)(2,1)}, bf16[8,1536,512]{2,1,0:T(8,128)(2,1)}, u32[]{:S(2)}, u32[]{:S(2)}) %collective-permute-start.1) | collective-permute-done | bytes 12582944 | tf_op jit(solution)/shard_map/ppermute | solution.py:54
  1661.7 11.2 gather_fusion.1
  1672.9 258.4 %collective-permute-done.2 = bf16[8,1536,512]{2,1,0:T(8,128)(2,1)} collective-permute-done((bf16[8,1536,512]{2,1,0:T(8,128)(2,1)}, bf16[8,1536,512]{2,1,0:T(8,128)(2,1)}, u32[]{:S(2)}, u32[]{:S(2)}) %collective-permute-start.2) | collective-permute-done | bytes 12582944 | tf_op jit(solution)/shard_map/ppermute | solution.py:54
  1931.4 11.2 gather_fusion.3
  1942.6 257.5 %collective-permute-done = bf16[8,512,1536]{2,1,0:T(8,128)(2,1)} collective-permute-done((bf16[8,512,1536]{2,1,0:T(8,128)(2,1)}, bf16[8,512,1536]{2,1,0:T(8,128)(2,1)}, u32[]{:S(2)}, u32[]{:S(2)}) %collective-permute-start) | collective-permute-done | bytes 12582944 | tf_op jit(solution)/shard_map/ppermute | solution.py:54
  2211.3 13.5 select_select_fusion.5
  2227.9 20.4 select_select_fusion.4
  2248.3 75.4 fusion.4
  2323.7 141.5 %fusion.8 = bf16[8,8,512,1536]{3,2,0,1:T(8,128)(2,1)} fusion(f32[8,512,8,512]{3,1,2,0:T(8,128)} %fusion.4, bf16[8,8,512,1536]{3,2,1,0:T(8,128)(2,1)} %bitcast.10, bf16[8,1536,512]{2,1,0:T(8,128)(2,1)} %get-tuple-element.35, bf16[8,512,1536]{2,1,0:T(8,128)(2,1)} %select_select_fusion.5), kind=kOutput, calls=%fused_computation.24 | convolution fusion | flops 103230210048 | bytes 293601280 | tf_op jit(solution)/shard_map/gsqf,sfd->gsqd/dot_general | solution.py:11
  2465.1 66.1 copy.44
  2550.8 34.0 reduce-window.16
  2591.6 30.7 scatter_custom_fusion.1
  2623.2 1002.8 %all-to-all-done.1 = bf16[8,4096,1536]{2,1,0:T(8,128)(2,1)} async-done(((bf16[8,4096,1536]{2,1,0:T(8,128)(2,1)}), bf16[8,4096,1536]{2,1,0:T(8,128)(2,1)}, u32[]{:S(2)}, u32[]{:S(2)}) %all-to-all-start.1) | async-done | bytes 100663328 | tf_op jit(solution)/shard_map/all_to_all | solution.py:33
  3626.0 175.1 %gather_fusion.4 = bf16[8192,1536]{1,0:T(8,128)(2,1)} fusion(bf16[32768,1536]{1,0:T(8,128)(2,1)} %bitcast.16, s32[8192]{0:T(1024)S(1)} %broadcast_clamp_fusion.1), kind=kCustom, calls=%fused_computation.3.clone | custom fusion | bytes 50364416 | tf_op jit(solution)/shard_map/jit(_take)/gather | solution.py:34
  3801.1 27.4 multiply_reduce_fusion.1
  3834.2 146.0 %gather_fusion.7 = bf16[32768,1536]{1,0:T(8,128)(2,1)} fusion(bf16[1025,1536]{1,0:T(8,128)(2,1)S(1)} %concatenate.7, s32[32768]{0:T(1024)S(1)} %fusion.43), kind=kCustom, calls=%fused_computation.8.clone | custom fusion | bytes 201457664 | tf_op jit(solution)/shard_map/jit(_take)/gather | solution.py:30
  3980.2 65.0 broadcast_select_fusion
  4061.0 1346.9 %collective-permute-done.4 = bf16[8,1536,512]{2,1,0:T(8,128)(2,1)} collective-permute-done((bf16[8,1536,512]{2,1,0:T(8,128)(2,1)}, bf16[8,1536,512]{2,1,0:T(8,128)(2,1)}, u32[]{:S(2)}, u32[]{:S(2)}) %collective-permute-start.4) | collective-permute-done | bytes 12582944 | tf_op jit(solution)/shard_map/ppermute | solution.py:54
  5418.7 258.9 %collective-permute-done.5 = bf16[8,1536,512]{2,1,0:T(8,128)(2,1)} collective-permute-done((bf16[8,1536,512]{2,1,0:T(8,128)(2,1)}, bf16[8,1536,512]{2,1,0:T(8,128)(2,1)}, u32[]{:S(2)}, u32[]{:S(2)}) %collective-permute-start.5) | collective-permute-done | bytes 12582944 | tf_op jit(solution)/shard_map/ppermute | solution.py:54
  5688.4 258.3 %collective-permute-done.3 = bf16[8,512,1536]{2,1,0:T(8,128)(2,1)} collective-permute-done((bf16[8,512,1536]{2,1,0:T(8,128)(2,1)}, bf16[8,512,1536]{2,1,0:T(8,128)(2,1)}, u32[]{:S(2)}, u32[]{:S(2)}) %collective-permute-start.3) | collective-permute-done | bytes 12582944 | tf_op jit(solution)/shard_map/ppermute | solution.py:54
  5957.4 13.5 select_select_fusion.2
  5974.0 20.4 select_select_fusion.1
  5994.4 75.4 fusion
  6069.8 141.4 %fusion.9 = bf16[8,8,512,1536]{3,2,0,1:T(8,128)(2,1)} fusion(f32[8,512,8,512]{3,1,2,0:T(8,128)} %fusion, bf16[8,8,512,1536]{3,2,1,0:T(8,128)(2,1)} %bitcast.28, bf16[8,1536,512]{2,1,0:T(8,128)(2,1)} %get-tuple-element.27, bf16[8,512,1536]{2,1,0:T(8,128)(2,1)} %select_select_fusion.2), kind=kOutput, calls=%fused_computation.25 | convolution fusion | flops 103230210048 | bytes 293601280 | tf_op jit(solution)/shard_map/gsqf,sfd->gsqd/dot_general | solution.py:11
  6211.2 66.1 copy.52
  6290.1 1081.9 %all-to-all-done.3 = bf16[8,4096,1536]{2,1,0:T(8,128)(2,1)} async-done(((bf16[8,4096,1536]{2,1,0:T(8,128)(2,1)}), bf16[8,4096,1536]{2,1,0:T(8,128)(2,1)}, u32[]{:S(2)}, u32[]{:S(2)}) %all-to-all-start.3) | async-done | bytes 100663328 | tf_op jit(solution)/shard_map/all_to_all | solution.py:33
  7372.0 175.0 %gather_fusion.9 = bf16[8192,1536]{1,0:T(8,128)(2,1)} fusion(bf16[32768,1536]{1,0:T(8,128)(2,1)} %bitcast.34, s32[8192]{0:T(1024)S(1)} %broadcast_clamp_fusion), kind=kCustom, calls=%fused_computation.9.clone | custom fusion | bytes 50364416 | tf_op jit(solution)/shard_map/jit(_take)/gather | solution.py:34
  7547.0 27.4 multiply_reduce_fusion
  (124 shorter events, 156.3 us)
Async XLA Ops:
  0.6 52.8 copy-start.14
  2.0 44.5 copy-start.15
  86.7 146.0 %copy-start.11 = (pred[32768]{0:T(1024)(128)(4,1)S(1)}, pred[32768]{0:T(1024)(128)(4,1)}, u32[]{:S(2)}) copy-start(pred[32768]{0:T(1024)(128)(4,1)} %compare_and_fusion.5) | copy-start | bytes 98308
  297.7 16.3 copy-start.24
  297.7 16.3 copy-start.21
  297.7 16.4 copy-start.17
  297.7 1950.6 %all-to-all-start = ((bf16[8,4096,1536]{2,1,0:T(8,128)(2,1)}), bf16[8,4096,1536]{2,1,0:T(8,128)(2,1)}, u32[]{:S(2)}, u32[]{:S(2)}) async-start(bf16[8,4096,1536]{2,1,0:T(8,128)(2,1)} %bitcast.9), calls=%async_computation | async-start | bytes 201326592 | tf_op jit(solution)/shard_map/all_to_all | solution.py:31
  308.7 1353.0 %collective-permute-start.1 = (bf16[8,1536,512]{2,1,0:T(8,128)(2,1)}, bf16[8,1536,512]{2,1,0:T(8,128)(2,1)}, u32[]{:S(2)}, u32[]{:S(2)}) collective-permute-start(bf16[8,1536,512]{2,1,0:T(8,128)(2,1)} %param.26), channel_id=1, source_target_pairs={{0,4},{1,5},{2,6},{3,7},{4,0},{5,1},{6,2},{7,3}} | collective-permute-start | bytes 37748744 | tf_op jit(solution)/shard_map/ppermute | solution.py:54
  312.0 1619.4 %collective-permute-start.2 = (bf16[8,1536,512]{2,1,0:T(8,128)(2,1)}, bf16[8,1536,512]{2,1,0:T(8,128)(2,1)}, u32[]{:S(2)}, u32[]{:S(2)}) collective-permute-start(bf16[8,1536,512]{2,1,0:T(8,128)(2,1)} %param.27), channel_id=1, source_target_pairs={{0,4},{1,5},{2,6},{3,7},{4,0},{5,1},{6,2},{7,3}} | collective-permute-start | bytes 37748744 | tf_op jit(solution)/shard_map/ppermute | solution.py:54
  312.0 1888.1 %collective-permute-start = (bf16[8,512,1536]{2,1,0:T(8,128)(2,1)}, bf16[8,512,1536]{2,1,0:T(8,128)(2,1)}, u32[]{:S(2)}, u32[]{:S(2)}) collective-permute-start(bf16[8,512,1536]{2,1,0:T(8,128)(2,1)} %param.28), channel_id=1, source_target_pairs={{0,4},{1,5},{2,6},{3,7},{4,0},{5,1},{6,2},{7,3}} | collective-permute-start | bytes 37748744 | tf_op jit(solution)/shard_map/ppermute | solution.py:54
  2211.3 16.6 copy-start
  2531.2 11.0 copy-start.8
  2531.2 11.7 copy-start.12
  2531.3 12.7 copy-start.5
  2531.3 15.7 copy-start.7
  2531.3 15.7 copy-start.16
  2531.3 1094.7 %all-to-all-start.1 = ((bf16[8,4096,1536]{2,1,0:T(8,128)(2,1)}), bf16[8,4096,1536]{2,1,0:T(8,128)(2,1)}, u32[]{:S(2)}, u32[]{:S(2)}) async-start(bf16[8,4096,1536]{2,1,0:T(8,128)(2,1)} %bitcast.15), calls=%async_computation.1 | async-start | bytes 201326592 | tf_op jit(solution)/shard_map/all_to_all | solution.py:33
  3801.1 27.4 copy-start.4
  3834.2 146.0 %copy-start.10 = (pred[32768]{0:T(1024)(128)(4,1)S(1)}, pred[32768]{0:T(1024)(128)(4,1)}, u32[]{:S(2)}) copy-start(pred[32768]{0:T(1024)(128)(4,1)} %compare_and_fusion.4) | copy-start | bytes 98308
  4045.2 15.0 copy-start.18
  4045.2 15.0 copy-start.20
  4045.2 15.1 copy-start.22
  4045.2 15.1 copy-start.23
  4045.3 1949.2 %all-to-all-start.2 = ((bf16[8,4096,1536]{2,1,0:T(8,128)(2,1)}), bf16[8,4096,1536]{2,1,0:T(8,128)(2,1)}, u32[]{:S(2)}, u32[]{:S(2)}) async-start(bf16[8,4096,1536]{2,1,0:T(8,128)(2,1)} %bitcast.27), calls=%async_computation.2 | async-start | bytes 201326592 | tf_op jit(solution)/shard_map/all_to_all | solution.py:31
  4056.2 1351.7 %collective-permute-start.4 = (bf16[8,1536,512]{2,1,0:T(8,128)(2,1)}, bf16[8,1536,512]{2,1,0:T(8,128)(2,1)}, u32[]{:S(2)}, u32[]{:S(2)}) collective-permute-start(bf16[8,1536,512]{2,1,0:T(8,128)(2,1)} %param.29), channel_id=1, source_target_pairs={{0,4},{1,5},{2,6},{3,7},{4,0},{5,1},{6,2},{7,3}} | collective-permute-start | bytes 37748744 | tf_op jit(solution)/shard_map/ppermute | solution.py:54
  4058.2 1619.4 %collective-permute-start.5 = (bf16[8,1536,512]{2,1,0:T(8,128)(2,1)}, bf16[8,1536,512]{2,1,0:T(8,128)(2,1)}, u32[]{:S(2)}, u32[]{:S(2)}) collective-permute-start(bf16[8,1536,512]{2,1,0:T(8,128)(2,1)} %param.30), channel_id=1, source_target_pairs={{0,4},{1,5},{2,6},{3,7},{4,0},{5,1},{6,2},{7,3}} | collective-permute-start | bytes 37748744 | tf_op jit(solution)/shard_map/ppermute | solution.py:54
  4058.3 1888.4 %collective-permute-start.3 = (bf16[8,512,1536]{2,1,0:T(8,128)(2,1)}, bf16[8,512,1536]{2,1,0:T(8,128)(2,1)}, u32[]{:S(2)}, u32[]{:S(2)}) collective-permute-start(bf16[8,512,1536]{2,1,0:T(8,128)(2,1)} %param.31), channel_id=1, source_target_pairs={{0,4},{1,5},{2,6},{3,7},{4,0},{5,1},{6,2},{7,3}} | collective-permute-start | bytes 37748744 | tf_op jit(solution)/shard_map/ppermute | solution.py:54
  5957.4 16.6 copy-start.1
  6277.3 11.0 copy-start.9
  6277.3 11.6 copy-start.13
  6277.3 1094.7 %all-to-all-start.3 = ((bf16[8,4096,1536]{2,1,0:T(8,128)(2,1)}), bf16[8,4096,1536]{2,1,0:T(8,128)(2,1)}, u32[]{:S(2)}, u32[]{:S(2)}) async-start(bf16[8,4096,1536]{2,1,0:T(8,128)(2,1)} %bitcast.33), calls=%async_computation.3 | async-start | bytes 201326592 | tf_op jit(solution)/shard_map/all_to_all | solution.py:33
  7547.0 27.4 copy-start.3
  (3 other events, 6.2 us)
where the time goes:
time: 7600 us; the launch traced here: 7580 us
  waiting for transfers between devices  5810 us (76%)
  local copies, waits for them, and re-layouts  926 us (12%)
  matrix products  434 us (6%)
  other arithmetic  355 us (5%)
    ppermute x6, waiting for transfers between devices, migrate_layer(): lax.ppermute(weight, 'ep', pairs)  3730 us
    all_to_all x2, waiting for transfers between devices, moe_layer(): lax.all_to_all(expert_out.reshape(group_size, slot_count * capacity, d_mo...  2080 us
    gather x2, local copies, waits for them, and re-layouts, moe_layer(): jnp.take(back_rows.reshape(group_size * slot_count * capacity, d_model),...  350 us
    gather x2, local copies, waits for them, and re-layouts, moe_layer(): jnp.take(padded, row_token, axis=0)  292 us
    dot_general x2, matrix products, expert_ffn(): jnp.einsum('gsqf,sfd->gsqd', inner, w_down, preferred_element_type=jnp.fl...  283 us
  transfers between devices with their start and end apart: 10, of which 8 were waited for; matrix products, arithmetic and copies ran while one was open for 3% of the time, Pallas kernels for 0%

commit v1 on v0

v1 whole, which is shorter than its diff:
```python
import jax
import jax.numpy as jnp
from jax import lax
from jax.experimental import pallas as pl
from jax.experimental.pallas import tpu as pltpu
from jax.sharding import PartitionSpec as P

CHUNKS = 4
TOK_BLOCK = 1024
ROW_TILE = 512


def dense_kernel(active_ref, x_ref, gate_ref, wg_ref, wu_ref, wd_ref, out_ref):
    slot = pl.program_id(1)
    tile_dev = ROW_TILE // gate_ref.shape[1]

    @pl.when(slot == 0)
    def _():
        out_ref[...] = jnp.zeros_like(out_ref)

    @pl.when(active_ref[slot] != 0)
    def _():
        def tile(step, carry):
            rows = pl.ds(pl.multiple_of(step * ROW_TILE, ROW_TILE), ROW_TILE)
            x = x_ref[rows, :]
            gate_act = jnp.dot(x, wg_ref[0], preferred_element_type=jnp.float32)
            up_act = jnp.dot(x, wu_ref[0], preferred_element_type=jnp.float32)
            inner = (gate_act * jax.nn.sigmoid(gate_act) * up_act).astype(jnp.bfloat16)
            gates = gate_ref[pl.ds(step * tile_dev, tile_dev)].reshape(ROW_TILE, gate_ref.shape[2])
            lane = lax.broadcasted_iota(jnp.int32, gates.shape, 1)
            gate = jnp.sum(jnp.where(lane == slot, gates, 0.0), axis=1, keepdims=True)
            expert_out = jnp.dot(inner, wd_ref[0], preferred_element_type=jnp.float32)
            expert_out = expert_out.astype(jnp.bfloat16).astype(jnp.float32)
            out_ref[rows, :] += jnp.where(gate != 0.0, gate * expert_out, 0.0)
            return carry

        lax.fori_loop(0, x_ref.shape[0] // ROW_TILE, tile, 0)


def dense_experts(x, gates, chunk, active, w_gate, w_up, w_down):
    rows, d_model = x.shape
    slots, _, d_ff = w_gate.shape
    group, tok_dev, _ = gates.shape
    per_dev = rows // group
    block_dev = TOK_BLOCK // per_dev
    return pl.pallas_call(
        dense_kernel,
        out_shape=jax.ShapeDtypeStruct((rows, d_model), jnp.float32),
        grid_spec=pltpu.PrefetchScalarGridSpec(
            num_scalar_prefetch=1,
            grid=(rows // TOK_BLOCK, slots),
            in_specs=[
                pl.BlockSpec((TOK_BLOCK, d_model), lambda t, s, a: (t, 0)),
                pl.BlockSpec((block_dev, per_dev, slots), lambda t, s, a: (t, chunk, 0)),
                pl.BlockSpec((1, d_model, d_ff), lambda t, s, a: (s, 0, 0)),
                pl.BlockSpec((1, d_model, d_ff), lambda t, s, a: (s, 0, 0)),
                pl.BlockSpec((1, d_ff, d_model), lambda t, s, a: (s, 0, 0)),
            ],
            out_specs=pl.BlockSpec((TOK_BLOCK, d_model), lambda t, s, a: (t, 0)),
        ),
        compiler_params=pltpu.CompilerParams(
            dimension_semantics=('arbitrary', 'arbitrary'), vmem_limit_bytes=60 * 1024 * 1024),
        cost_estimate=pl.CostEstimate(
            flops=rows * slots * 6 * d_model * d_ff, transcendentals=rows * slots * d_ff,
            bytes_accessed=rows * d_model * 6 + (rows // TOK_BLOCK) * slots * 6 * d_model * d_ff),
        name='dense_experts',
    )(active, x, gates, w_gate, w_up, w_down)


def add_kernel(hidden_ref, mixed_ref, out_ref):
    out_ref[...] = (hidden_ref[...].astype(jnp.float32) + mixed_ref[...]).astype(out_ref.dtype)


def add_mixed(hidden, mixed):
    return pl.pallas_call(
        add_kernel,
        out_shape=jax.ShapeDtypeStruct(hidden.shape, hidden.dtype),
        cost_estimate=pl.CostEstimate(flops=2_000_000, transcendentals=0, bytes_accessed=hidden.size * 8),
        name='add_mixed',
    )(hidden, mixed)


def place_kernel(own_idx, in_idx, changed, *refs):
    own, incoming, outs = refs[0:3], refs[3:6], refs[6:9]
    slot = pl.program_id(0)

    @pl.when(changed[slot] != 0)
    def _():
        for src, dst in zip(incoming, outs):
            dst[...] = src[...]

    @pl.when(changed[slot] == 0)
    def _():
        for src, dst in zip(own, outs):
            dst[...] = src[...]


def place_layer(own, incoming, source, changed):
    slots = own[0].shape[0]
    own_idx = jnp.where(changed, 0, jnp.arange(slots)).astype(jnp.int32)
    in_idx = jnp.where(changed, source, 0).astype(jnp.int32)

    def block(weight):
        return (1,) + weight.shape[1:]

    return pl.pallas_call(
        place_kernel,
        out_shape=[jax.ShapeDtypeStruct(w.shape, w.dtype) for w in own],
        grid_spec=pltpu.PrefetchScalarGridSpec(
            num_scalar_prefetch=3,
            grid=(slots,),
            in_specs=[pl.BlockSpec(block(w), lambda s, o, i, c: (o[s], 0, 0)) for w in own]
            + [pl.BlockSpec(block(w), lambda s, o, i, c: (i[s], 0, 0)) for w in own],
            out_specs=[pl.BlockSpec(block(w), lambda s, o, i, c: (s, 0, 0)) for w in own],
        ),
        compiler_params=pltpu.CompilerParams(
            dimension_semantics=('arbitrary',), vmem_limit_bytes=60 * 1024 * 1024),
        cost_estimate=pl.CostEstimate(
            flops=30_000_000, transcendentals=0, bytes_accessed=2 * sum(w.size * 2 for w in own)),
        name='place_slots',
    )(own_idx, in_idx, changed.astype(jnp.int32), *own, *incoming)


def first_holder(row):
    same = row[:, None] == row[None, :]
    index = jnp.arange(row.shape[0])
    return ~jnp.any(same & (index[None, :] < index[:, None]), axis=1)


def solution(mesh):
    group = mesh.shape['ep']
    tok_spec = P(('replica', 'ep'), None)
    slot_spec = P('ep', None, None)
    map_spec = P(None, None)

    def body(hidden, route_one, gate_one, route_two, gate_two, w_gate_one, w_up_one, w_down_one,
             w_gate_two, w_up_two, w_down_two, old_map, new_map):
        device = lax.axis_index('ep')
        tok_dev, top = route_one.shape
        slots = w_gate_one.shape[0]
        per_chunk = tok_dev // CHUNKS
        weights = ((w_gate_one, w_up_one, w_down_one), (w_gate_two, w_up_two, w_down_two))

        def gather_chunk(rows):
            return lax.all_gather(rows, 'ep', axis=0, tiled=True)

        packed = jnp.concatenate(
            [route_one.T.astype(jnp.float32), gate_one.T, route_two.T.astype(jnp.float32), gate_two.T], axis=0)
        packed = lax.all_gather(packed, 'ep', axis=0, tiled=False)

        gates, actives, dests, placements = [], [], [], []
        for layer in range(2):
            old_row, new_row = old_map[layer], new_map[layer]
            mine = lax.dynamic_slice(old_row, (device * slots,), (slots,))
            active = lax.dynamic_slice(first_holder(old_row), (device * slots,), (slots,))
            route = packed[:, 2 * layer * top:(2 * layer + 1) * top, :]
            gate = packed[:, (2 * layer + 1) * top:(2 * layer + 2) * top, :]
            hit = (route[:, None] == mine.astype(jnp.float32)[None, :, None, None]) & active[None, :, None, None]
            local = jnp.sum(jnp.where(hit, gate[:, None], 0.0), axis=2)
            gates.append(local.transpose(0, 2, 1))
            actives.append(active.astype(jnp.int32))
            dests.append((jnp.argmax(old_row != new_row) // slots).astype(jnp.int32))
            from_dev = (device + group // 2) % group
            old_from = lax.dynamic_slice(old_row, (from_dev * slots,), (slots,))
            new_mine = lax.dynamic_slice(new_row, (device * slots,), (slots,))
            source = jnp.argmax(new_mine[:, None] == old_from[None, :], axis=1)
            placements.append((source, mine != new_mine))

        def compute(layer, chunk, rows):
            return dense_experts(rows, gates[layer], chunk, actives[layer], *weights[layer])

        def compute_and_send(layer, chunk, rows, weight):
            def branch(dest):
                def run(rows, weight):
                    pair = [((dest + group // 2) % group, dest)]
                    return compute(layer, chunk, rows), lax.ppermute(weight, 'ep', pair)
                return run
            return lax.switch(dests[layer], [branch(dest) for dest in range(group)], rows, weight)

        incoming = [[], []]
        states = [hidden[chunk * per_chunk:(chunk + 1) * per_chunk] for chunk in range(CHUNKS)]
        for layer in range(2):
            gathered = [gather_chunk(rows) for rows in states]
            for chunk in range(CHUNKS):
                if chunk < 3:
                    partial, moved = compute_and_send(layer, chunk, gathered[chunk], weights[layer][chunk])
                    incoming[layer].append(moved)
                else:
                    partial = compute(layer, chunk, gathered[chunk])
                mixed = lax.psum_scatter(partial, 'ep', scatter_dimension=0, tiled=True)
                states[chunk] = add_mixed(states[chunk], mixed)
        hidden_out = jnp.concatenate(states, axis=0)
        placed = [place_layer(weights[layer], incoming[layer], *placements[layer]) for layer in range(2)]
        return (hidden_out, *placed[0], *placed[1])

    in_specs = (tok_spec,) * 5 + (slot_spec,) * 6 + (map_spec, map_spec)
    out_specs = (tok_spec,) + (slot_spec,) * 6
    return jax.shard_map(body, mesh=mesh, in_specs=in_specs, out_specs=out_specs, check_vma=False)
```

time: 7600 us -> 1700 us (0.22)
  waiting for transfers between devices: 5810 us -> 768 us
  local copies, waits for them, and re-layouts: 926 us -> 13.6 us
  Pallas kernels: 0 us -> 824 us
  matrix products: 434 us -> 0 us
  other arithmetic: 355 us -> 13.7 us
    ppermute x6, waiting for transfers between devices: 3730 us -> 305 us  [run(): return (compute(layer, chunk, rows), lax.ppermute(weight, 'ep', pair))]
    all_to_all x4 -> x0, waiting for transfers between devices: 2080 us -> none  [the longest x2 2080 us: moe_layer(): lax.all_to_all(expert_out.reshape(group_size, slot_count * capacity, d_mo...]
    pallas_call x0 -> x18, Pallas kernels: none -> 824 us  [the longest x8 749 us: dense_experts(): pl.pallas_call(dense_kernel, out_shape=jax.ShapeDtypeStruct((rows, d_mode...]
    gather x10 -> x0, local copies, waits for them, and re-layouts: 708 us -> none  [the longest x2 350 us: moe_layer(): jnp.take(back_rows.reshape(group_size * slot_count * capacity, d_model),...]
    dot_general x4 -> x0, matrix products: 434 us -> none  [the longest x2 283 us: expert_ffn(): jnp.einsum('gsqf,sfd->gsqd', inner, w_down, preferred_element_type=jnp.fl...]
    reduce_scatter x0 -> x8, waiting for transfers between devices: none -> 378 us  [body(): mixed = lax.psum_scatter(partial, 'ep', scatter_dimension=0, tiled=True)]
    select_n x13 -> x2, other arithmetic: 199 us -> 1.04 us  [place_layer(): in_idx = jnp.where(changed, source, 0).astype(jnp.int32)]
    convert_element_type x2 -> x0, local copies, waits for them, and re-layouts: 132 us -> none  [expert_ffn(): jnp.einsum('gsqf,sfd->gsqd', inner, w_down, preferred_element_type=jnp.fl...]
  transfers between devices with their start and end apart: 10 -> 23, of which waited for: 8 -> 9; matrix products, arithmetic and copies ran while one was open for 3% -> 1% of each run, Pallas kernels for 0% -> 49%
where the time goes in v1:
time: 1700 us; the launch traced here: 1690 us
  Pallas kernels  824 us (48%)
  waiting for transfers between devices  768 us (45%)
  loops' own time  27.3 us (2%)
  starting transfers between devices  20.5 us (1%)
  between operations  19.9 us (1%)
    pallas_call x8, Pallas kernels, dense_experts(): pl.pallas_call(dense_kernel, out_shape=jax.ShapeDtypeStruct((rows, d_mode...  749 us
    reduce_scatter x8, waiting for transfers between devices, body(): mixed = lax.psum_scatter(partial, 'ep', scatter_dimension=0, tiled=True)  378 us
    ppermute x6, waiting for transfers between devices, run(): return (compute(layer, chunk, rows), lax.ppermute(weight, 'ep', pair))  305 us
    all_gather x8, waiting for transfers between devices, gather_chunk(): return lax.all_gather(rows, 'ep', axis=0, tiled=True)  70.4 us
    pallas_call x2, Pallas kernels, place_layer(): pl.pallas_call(place_kernel, out_shape=[jax.ShapeDtypeStruct(w.shape, w.d...  53.7 us
  transfers between devices with their start and end apart: 23, of which 9 were waited for; matrix products, arithmetic and copies ran while one was open for 1% of the time, Pallas kernels for 49%

profile of v1, /device:TPU:0, one launch (start us, length us, event | category | flops | bytes accessed | tf_op | source)
XLA Modules:
  0.0 1687.3 jit_solution(12720345792339157920)
XLA Ops:
  9.5 3.6 fusion.22
  17.3 13.5 all-gather.27.cloned.1.call-done
  36.5 35.7 %all-gather.23.cloned.1.call-done.x_ref = bf16[2048,1536]{1,0:T(8,128)(2,1)} async-done(((bf16[256,1536]{1,0:T(8,128)(2,1)}), bf16[2048,1536]{1,0:T(8,128)(2,1)}) %all-gather.23.cloned.1.call-update) | async-done | bytes 6291472 | tf_op jit(solution)/shard_map/all_gather | solution.py:145
  72.2 93.6 %dense_experts.98 = f32[2048,1536]{1,0:T(8,128)} custom-call(s32[8]{0:T(128)S(1)} %get-tuple-element.923.active_ref, bf16[2048,1536]{1,0:T(8,128)(2,1)} %all-gather.23.cloned.1.call-done.x_ref, f32[8,1024,8]{2,1,0:T(8,128)} %bitcast.68, bf16[8,1536,512]{2,1,0:T(8,128)(2,1)} %refs_0_.2, bf16[8,1536,512]{2,1,0:T(8,128)(2,1)} %refs_1_.2, ...), custom_call_target="tpu_custom_call" | custom-call | flops 77309411328 | bytes 94371840 | tf_op jit(solution)/shard_map/dense_experts/pallas_call | solution.py:46
  169.8 99.1 %conditional.6 = (f32[2048,1536]{1,0:T(8,128)}, bf16[8,1536,512]{2,1,0:T(8,128)(2,1)}) conditional(s32[]{:T(128)} %clamp.4, (s32[8]{0:T(128)S(1)}, bf16[2048,1536]{1,0:T(8,128)(2,1)}, f32[8,1024,8]{2,1,0:T(8,128)}, bf16[8,1536,512]{2,1,0:T(8,128)(2,1)}, bf16[8,1536,512]{2,1,0:T(8,128)(2,1)}, ...), branch_computations={%region_3.4_spmd, %region_4.5_spmd, %region_5.6_spmd, %region_6.7_... | conditional | flops 77309411328 | bytes 144703536 | solution.py:178
  169.8 5.3 collective-permute-start.1
  175.1 93.6 %dense_experts.51 = f32[2048,1536]{1,0:T(8,128)} custom-call(s32[8]{0:T(128)S(1)} %get-tuple-element.582.active_ref, bf16[2048,1536]{1,0:T(8,128)(2,1)} %get-tuple-element.583.x_ref, f32[8,1024,8]{2,1,0:T(8,128)} %get-tuple-element.584.gate_ref, bf16[8,1536,512]{2,1,0:T(8,128)(2,1)} %get-tuple-element.585.wg_ref, ...), custom_call_target="tpu_custom_call" | custom-call | flops 77309411328 | bytes 94371840 | tf_op jit(solution)/shard_map/cond/branch_1_fun/dense_experts/pallas_call | solution.py:46
  269.1 108.9 %conditional.10 = (f32[2048,1536]{1,0:T(8,128)}, bf16[8,512,1536]{2,1,0:T(8,128)(2,1)}) conditional(s32[]{:T(128)} %clamp.4, (s32[8]{0:T(128)S(1)}, bf16[2048,1536]{1,0:T(8,128)(2,1)}, f32[8,1024,8]{2,1,0:T(8,128)}, bf16[8,1536,512]{2,1,0:T(8,128)(2,1)}, bf16[8,1536,512]{2,1,0:T(8,128)(2,1)}, ...), branch_computations={%region_42.43_spmd, %region_43.44_spmd, %region_44.45_spmd, %regio... | conditional | flops 77309411328 | bytes 144703536 | solution.py:178
  269.1 5.2 collective-permute-start.33
  274.3 93.6 %dense_experts.83 = f32[2048,1536]{1,0:T(8,128)} custom-call(s32[8]{0:T(128)S(1)} %get-tuple-element.774.active_ref, bf16[2048,1536]{1,0:T(8,128)(2,1)} %get-tuple-element.775.x_ref, f32[8,1024,8]{2,1,0:T(8,128)} %get-tuple-element.776.gate_ref, bf16[8,1536,512]{2,1,0:T(8,128)(2,1)} %get-tuple-element.777.wg_ref, ...), custom_call_target="tpu_custom_call" | custom-call | flops 77309411328 | bytes 94371840 | tf_op jit(solution)/shard_map/cond/branch_1_fun/dense_experts/pallas_call | solution.py:46
  378.1 106.6 %conditional.8 = (f32[2048,1536]{1,0:T(8,128)}, bf16[8,1536,512]{2,1,0:T(8,128)(2,1)}) conditional(s32[]{:T(128)} %clamp.4, (s32[8]{0:T(128)S(1)}, bf16[2048,1536]{1,0:T(8,128)(2,1)}, f32[8,1024,8]{2,1,0:T(8,128)}, bf16[8,1536,512]{2,1,0:T(8,128)(2,1)}, bf16[8,1536,512]{2,1,0:T(8,128)(2,1)}, ...), branch_computations={%region_24.25_spmd, %region_25.26_spmd, %region_26.27_spmd, %regio... | conditional | flops 77309411328 | bytes 144703536 | solution.py:178
  378.1 5.2 collective-permute-start.17
  383.3 93.6 %dense_experts.67 = f32[2048,1536]{1,0:T(8,128)} custom-call(s32[8]{0:T(128)S(1)} %get-tuple-element.678.active_ref, bf16[2048,1536]{1,0:T(8,128)(2,1)} %get-tuple-element.679.x_ref, f32[8,1024,8]{2,1,0:T(8,128)} %get-tuple-element.680.gate_ref, bf16[8,1536,512]{2,1,0:T(8,128)(2,1)} %get-tuple-element.681.wg_ref, ...), custom_call_target="tpu_custom_call" | custom-call | flops 77309411328 | bytes 94371840 | tf_op jit(solution)/shard_map/cond/branch_1_fun/dense_experts/pallas_call | solution.py:46
  484.8 2.7 add_mixed.14.hidden_ref
  490.4 192.0 %reduce-scatter.17.cloned.1.call-done.mixed_ref = f32[256,1536]{1,0:T(8,128)} async-done(((f32[2048,1536]{1,0:T(8,128)}), f32[256,1536]{1,0:T(8,128)}) %reduce-scatter.17.cloned.1.call-update) | async-done | bytes 1572880 | tf_op jit(solution)/shard_map/reduce_scatter | solution.py:190
  685.1 170.4 %reduce-scatter.13.cloned.1.call-done.mixed_ref = f32[256,1536]{1,0:T(8,128)} async-done(((f32[2048,1536]{1,0:T(8,128)}), f32[256,1536]{1,0:T(8,128)}) %reduce-scatter.13.cloned.1.call-update) | async-done | bytes 1572880 | tf_op jit(solution)/shard_map/reduce_scatter | solution.py:190
  862.1 34.6 %all-gather.25.cloned.1.call-done.x_ref = bf16[2048,1536]{1,0:T(8,128)(2,1)} async-done(((bf16[256,1536]{1,0:T(8,128)(2,1)}), bf16[2048,1536]{1,0:T(8,128)(2,1)}) %all-gather.25.cloned.1.call-update) | async-done | bytes 6291472 | tf_op jit(solution)/shard_map/all_gather | solution.py:145
  896.7 93.6 %dense_experts.99 = f32[2048,1536]{1,0:T(8,128)} custom-call(s32[8]{0:T(128)S(1)} %get-tuple-element.921.active_ref, bf16[2048,1536]{1,0:T(8,128)(2,1)} %all-gather.25.cloned.1.call-done.x_ref, f32[8,1024,8]{2,1,0:T(8,128)} %bitcast.43, bf16[8,1536,512]{2,1,0:T(8,128)(2,1)} %refs_0_.3, bf16[8,1536,512]{2,1,0:T(8,128)(2,1)} %refs_1_.3, ...), custom_call_target="tpu_custom_call" | custom-call | flops 77309411328 | bytes 94371840 | tf_op jit(solution)/shard_map/dense_experts/pallas_call | solution.py:46
  994.3 208.1 %conditional.7 = (f32[2048,1536]{1,0:T(8,128)}, bf16[8,1536,512]{2,1,0:T(8,128)(2,1)}) conditional(s32[]{:T(128)} %clamp.5, (s32[8]{0:T(128)S(1)}, bf16[2048,1536]{1,0:T(8,128)(2,1)}, f32[8,1024,8]{2,1,0:T(8,128)}, bf16[8,1536,512]{2,1,0:T(8,128)(2,1)}, bf16[8,1536,512]{2,1,0:T(8,128)(2,1)}, ...), branch_computations={%region_15.16_spmd, %region_16.17_spmd, %region_17.18_spmd, %regio... | conditional | flops 77309411328 | bytes 144703536 | solution.py:178
  995.6 93.6 %dense_experts.58 = f32[2048,1536]{1,0:T(8,128)} custom-call(s32[8]{0:T(128)S(1)} %get-tuple-element.624.active_ref, bf16[2048,1536]{1,0:T(8,128)(2,1)} %get-tuple-element.625.x_ref, f32[8,1024,8]{2,1,0:T(8,128)} %get-tuple-element.626.gate_ref, bf16[8,1536,512]{2,1,0:T(8,128)(2,1)} %get-tuple-element.627.wg_ref, ...), custom_call_target="tpu_custom_call" | custom-call | flops 77309411328 | bytes 94371840 | tf_op jit(solution)/shard_map/cond/branch_0_fun/dense_experts/pallas_call | solution.py:46
  1089.2 112.8 %collective-permute-done.8 = bf16[8,1536,512]{2,1,0:T(8,128)(2,1)} collective-permute-done((bf16[8,1536,512]{2,1,0:T(8,128)(2,1)}, bf16[8,1536,512]{2,1,0:T(8,128)(2,1)}, u32[]{:S(2)}, u32[]{:S(2)}) %collective-permute-start.8) | collective-permute-done | bytes 12582944 | tf_op jit(solution)/shard_map/cond/branch_0_fun/ppermute | solution.py:176
  1202.5 191.0 %conditional.11 = (f32[2048,1536]{1,0:T(8,128)}, bf16[8,512,1536]{2,1,0:T(8,128)(2,1)}) conditional(s32[]{:T(128)} %clamp.5, (s32[8]{0:T(128)S(1)}, bf16[2048,1536]{1,0:T(8,128)(2,1)}, f32[8,1024,8]{2,1,0:T(8,128)}, bf16[8,1536,512]{2,1,0:T(8,128)(2,1)}, bf16[8,1536,512]{2,1,0:T(8,128)(2,1)}, ...), branch_computations={%region_51.52_spmd, %region_52.53_spmd, %region_53.54_spmd, %regio... | conditional | flops 77309411328 | bytes 144703536 | solution.py:178
  1203.8 93.6 %dense_experts.90 = f32[2048,1536]{1,0:T(8,128)} custom-call(s32[8]{0:T(128)S(1)} %get-tuple-element.816.active_ref, bf16[2048,1536]{1,0:T(8,128)(2,1)} %get-tuple-element.817.x_ref, f32[8,1024,8]{2,1,0:T(8,128)} %get-tuple-element.818.gate_ref, bf16[8,1536,512]{2,1,0:T(8,128)(2,1)} %get-tuple-element.819.wg_ref, ...), custom_call_target="tpu_custom_call" | custom-call | flops 77309411328 | bytes 94371840 | tf_op jit(solution)/shard_map/cond/branch_0_fun/dense_experts/pallas_call | solution.py:46
  1297.4 96.0 %collective-permute-done.40 = bf16[8,512,1536]{2,1,0:T(8,128)(2,1)} collective-permute-done((bf16[8,512,1536]{2,1,0:T(8,128)(2,1)}, bf16[8,512,1536]{2,1,0:T(8,128)(2,1)}, u32[]{:S(2)}, u32[]{:S(2)}) %collective-permute-start.40) | collective-permute-done | bytes 12582944 | tf_op jit(solution)/shard_map/cond/branch_0_fun/ppermute | solution.py:176
  1393.7 199.6 %conditional.9 = (f32[2048,1536]{1,0:T(8,128)}, bf16[8,1536,512]{2,1,0:T(8,128)(2,1)}) conditional(s32[]{:T(128)} %clamp.5, (s32[8]{0:T(128)S(1)}, bf16[2048,1536]{1,0:T(8,128)(2,1)}, f32[8,1024,8]{2,1,0:T(8,128)}, bf16[8,1536,512]{2,1,0:T(8,128)(2,1)}, bf16[8,1536,512]{2,1,0:T(8,128)(2,1)}, ...), branch_computations={%region_33.34_spmd, %region_34.35_spmd, %region_35.36_spmd, %regio... | conditional | flops 77309411328 | bytes 144703536 | solution.py:178
  1395.0 93.6 %dense_experts.74 = f32[2048,1536]{1,0:T(8,128)} custom-call(s32[8]{0:T(128)S(1)} %get-tuple-element.720.active_ref, bf16[2048,1536]{1,0:T(8,128)(2,1)} %get-tuple-element.721.x_ref, f32[8,1024,8]{2,1,0:T(8,128)} %get-tuple-element.722.gate_ref, bf16[8,1536,512]{2,1,0:T(8,128)(2,1)} %get-tuple-element.723.wg_ref, ...), custom_call_target="tpu_custom_call" | custom-call | flops 77309411328 | bytes 94371840 | tf_op jit(solution)/shard_map/cond/branch_0_fun/dense_experts/pallas_call | solution.py:46
  1488.6 96.0 %collective-permute-done.24 = bf16[8,1536,512]{2,1,0:T(8,128)(2,1)} collective-permute-done((bf16[8,1536,512]{2,1,0:T(8,128)(2,1)}, bf16[8,1536,512]{2,1,0:T(8,128)(2,1)}, u32[]{:S(2)}, u32[]{:S(2)}) %collective-permute-start.24) | collective-permute-done | bytes 12582944 | tf_op jit(solution)/shard_map/cond/branch_0_fun/ppermute | solution.py:176
  1597.6 26.8 %place_slots.2 = (bf16[8,1536,512]{2,1,0:T(8,128)(2,1)}, bf16[8,1536,512]{2,1,0:T(8,128)(2,1)}, bf16[8,512,1536]{2,1,0:T(8,128)(2,1)}) custom-call(s32[8]{0:T(128)} %get-tuple-element.944.own_idx, s32[8]{0:T(128)} %get-tuple-element.943.in_idx, s32[8]{0:T(128)} %get-tuple-element.918.changed, bf16[8,1536,512]{2,1,0:T(8,128)(2,1)} %refs_0_.2, ...), custom_call_target="tpu_custom_call" | custom-call | flops 30000000 | bytes 75497472 | tf_op jit(solution)/shard_map/place_slots/pallas_call | solution.py:106
  1624.4 26.9 %place_slots.3 = (bf16[8,1536,512]{2,1,0:T(8,128)(2,1)}, bf16[8,1536,512]{2,1,0:T(8,128)(2,1)}, bf16[8,512,1536]{2,1,0:T(8,128)(2,1)}) custom-call(s32[8]{0:T(128)} %get-tuple-element.940.own_idx, s32[8]{0:T(128)} %get-tuple-element.939.in_idx, s32[8]{0:T(128)} %get-tuple-element.915.changed, bf16[8,1536,512]{2,1,0:T(8,128)(2,1)} %refs_0_.3, ...), custom_call_target="tpu_custom_call" | custom-call | flops 30000000 | bytes 75497472 | tf_op jit(solution)/shard_map/place_slots/pallas_call | solution.py:106
  1651.2 2.7 add_mixed.15
  1659.3 15.3 reduce-scatter.15.cloned.1.call-done.mixed_ref
  1677.2 3.1 pad_maximum_fusion
  (110 shorter events, 43.6 us)
Async XLA Ops:
  7.2 23.6 %all-gather.27.cloned.1.call-start = ((), (), s32[]{:S(2)}) async-start(), calls=%async_computation.24 | async-start | bytes 1179648 | tf_op jit(solution)/shard_map/all_gather | solution.py:149
  9.5 62.7 %all-gather.23.cloned.1.call-start = ((), (), s32[]{:S(2)}) async-start(), calls=%async_computation.20 | async-start | bytes 7077888 | tf_op jit(solution)/shard_map/all_gather | solution.py:145
  13.1 156.7 %all-gather.11.cloned.1.call-start = ((), (), s32[]{:S(2)}) async-start(), calls=%async_computation.8 | async-start | bytes 7077888 | tf_op jit(solution)/shard_map/all_gather | solution.py:145
  13.8 255.2 %all-gather.19.cloned.1.call-start = ((), (), s32[]{:S(2)}) async-start(), calls=%async_computation.16 | async-start | bytes 7077888 | tf_op jit(solution)/shard_map/all_gather | solution.py:145
  14.4 363.7 %all-gather.15.cloned.1.call-start = ((), (), s32[]{:S(2)}) async-start(), calls=%async_computation.12 | async-start | bytes 7077888 | tf_op jit(solution)/shard_map/all_gather | solution.py:145
  15.0 469.8 %reduce-scatter.21.cloned.1.call-start = ((), (), s32[]{:S(2)}) async-start(), calls=%async_computation.21 | async-start | bytes 14155776 | tf_op jit(solution)/shard_map/reduce_scatter | solution.py:190
  15.8 17.0 %copy-start.2 = (s32[1,64]{1,0:T(1,128)}, s32[1,64]{1,0:T(1,128)S(1)}, u32[]{:S(2)}) copy-start(s32[1,64]{1,0:T(1,128)S(1)} %get-tuple-element.938) | copy-start | bytes 772
  15.8 17.0 %copy-start.4 = (s32[1,64]{1,0:T(1,128)}, s32[1,64]{1,0:T(1,128)S(1)}, u32[]{:S(2)}) copy-start(s32[1,64]{1,0:T(1,128)S(1)} %get-tuple-element.935) | copy-start | bytes 772
  165.9 321.7 %reduce-scatter.9.cloned.1.call-start = ((), (), s32[]{:S(2)}) async-start(), calls=%async_computation.9 | async-start | bytes 14155776 | tf_op jit(solution)/shard_map/reduce_scatter | solution.py:190
  169.8 98.9 %collective-permute-start.1 = (bf16[8,1536,512]{2,1,0:T(8,128)(2,1)}, bf16[8,1536,512]{2,1,0:T(8,128)(2,1)}, u32[]{:S(2)}, u32[]{:S(2)}) collective-permute-start(bf16[8,1536,512]{2,1,0:T(8,128)(2,1)} %get-tuple-element.585.wg_ref), channel_id=1, source_target_pairs={{5,1}} | collective-permute-start | bytes 37748744 | tf_op jit(solution)/shard_map/cond/branch_1_fun/ppermute | solution.py:176
  269.0 413.4 %reduce-scatter.17.cloned.1.call-start = ((), (), s32[]{:S(2)}) async-start(), calls=%async_computation.17 | async-start | bytes 14155776 | tf_op jit(solution)/shard_map/reduce_scatter | solution.py:190
  269.1 98.9 %collective-permute-start.33 = (bf16[8,512,1536]{2,1,0:T(8,128)(2,1)}, bf16[8,512,1536]{2,1,0:T(8,128)(2,1)}, u32[]{:S(2)}, u32[]{:S(2)}) collective-permute-start(bf16[8,512,1536]{2,1,0:T(8,128)(2,1)} %get-tuple-element.779.wd_ref), channel_id=1, source_target_pairs={{5,1}} | collective-permute-start | bytes 37748744 | tf_op jit(solution)/shard_map/cond/branch_1_fun/ppermute | solution.py:176
  378.0 477.4 %reduce-scatter.13.cloned.1.call-start = ((), (), s32[]{:S(2)}) async-start(), calls=%async_computation.13 | async-start | bytes 14155776 | tf_op jit(solution)/shard_map/reduce_scatter | solution.py:190
  378.1 98.8 %collective-permute-start.17 = (bf16[8,1536,512]{2,1,0:T(8,128)(2,1)}, bf16[8,1536,512]{2,1,0:T(8,128)(2,1)}, u32[]{:S(2)}, u32[]{:S(2)}) collective-permute-start(bf16[8,1536,512]{2,1,0:T(8,128)(2,1)} %get-tuple-element.682.wu_ref), channel_id=1, source_target_pairs={{5,1}} | collective-permute-start | bytes 37748744 | tf_op jit(solution)/shard_map/cond/branch_1_fun/ppermute | solution.py:176
  484.7 373.7 %copy-start.14 = (pred[64]{0:T(512)(128)(4,1)S(1)}, pred[64]{0:T(512)(128)(4,1)}, u32[]{:S(2)}) copy-start(pred[64]{0:T(512)(128)(4,1)} %get-tuple-element.948) | copy-start | bytes 196
  484.7 373.8 %copy-start = (f32[8,8,1024]{2,1,0:T(8,128)S(1)}, f32[8,8,1024]{2,1,0:T(8,128)}, u32[]{:S(2)}) copy-start(f32[8,8,1024]{2,1,0:T(8,128)} %get-tuple-element.929) | copy-start | bytes 786436
  484.7 373.8 %copy-start.1 = (f32[8,8,1024]{2,1,0:T(8,128)S(1)}, f32[8,8,1024]{2,1,0:T(8,128)}, u32[]{:S(2)}) copy-start(f32[8,8,1024]{2,1,0:T(8,128)} %get-tuple-element.930) | copy-start | bytes 786436
  484.7 373.8 %copy-start.11 = (f32[8]{0:T(128)S(1)}, f32[8]{0:T(128)}, u32[]{:S(2)}) copy-start(f32[8]{0:T(128)} %get-tuple-element.949) | copy-start | bytes 100
  484.7 411.9 %all-gather.25.cloned.1.call-start = ((), (), s32[]{:S(2)}) async-start(), calls=%async_computation.22 | async-start | bytes 7077888 | tf_op jit(solution)/shard_map/all_gather | solution.py:145
  487.5 506.8 %all-gather.13.cloned.1.call-start = ((), (), s32[]{:S(2)}) async-start(), calls=%async_computation.10 | async-start | bytes 7077888 | tf_op jit(solution)/shard_map/all_gather | solution.py:145
  490.3 712.2 %all-gather.21.cloned.1.call-start = ((), (), s32[]{:S(2)}) async-start(), calls=%async_computation.18 | async-start | bytes 7077888 | tf_op jit(solution)/shard_map/all_gather | solution.py:145
  685.0 708.6 %all-gather.17.cloned.1.call-start = ((), (), s32[]{:S(2)}) async-start(), calls=%async_computation.14 | async-start | bytes 7077888 | tf_op jit(solution)/shard_map/all_gather | solution.py:145
  858.2 793.1 %reduce-scatter.23.cloned.1.call-start = ((), (), s32[]{:S(2)}) async-start(), calls=%async_computation.23 | async-start | bytes 14155776 | tf_op jit(solution)/shard_map/reduce_scatter | solution.py:190
  990.4 663.6 %reduce-scatter.11.cloned.1.call-start = ((), (), s32[]{:S(2)}) async-start(), calls=%async_computation.11 | async-start | bytes 14155776 | tf_op jit(solution)/shard_map/reduce_scatter | solution.py:190
  994.3 207.7 %collective-permute-start.8 = (bf16[8,1536,512]{2,1,0:T(8,128)(2,1)}, bf16[8,1536,512]{2,1,0:T(8,128)(2,1)}, u32[]{:S(2)}, u32[]{:S(2)}) collective-permute-start(bf16[8,1536,512]{2,1,0:T(8,128)(2,1)} %get-tuple-element.627.wg_ref), channel_id=1, source_target_pairs={{4,0}} | collective-permute-start | bytes 37748744 | tf_op jit(solution)/shard_map/cond/branch_0_fun/ppermute | solution.py:176
  1202.5 454.2 %reduce-scatter.19.cloned.1.call-start = ((), (), s32[]{:S(2)}) async-start(), calls=%async_computation.19 | async-start | bytes 14155776 | tf_op jit(solution)/shard_map/reduce_scatter | solution.py:190
  1202.5 190.8 %collective-permute-start.40 = (bf16[8,512,1536]{2,1,0:T(8,128)(2,1)}, bf16[8,512,1536]{2,1,0:T(8,128)(2,1)}, u32[]{:S(2)}, u32[]{:S(2)}) collective-permute-start(bf16[8,512,1536]{2,1,0:T(8,128)(2,1)} %get-tuple-element.821.wd_ref), channel_id=1, source_target_pairs={{4,0}} | collective-permute-start | bytes 37748744 | tf_op jit(solution)/shard_map/cond/branch_0_fun/ppermute | solution.py:176
  1393.6 281.0 %reduce-scatter.15.cloned.1.call-start = ((), (), s32[]{:S(2)}) async-start(), calls=%async_computation.15 | async-start | bytes 14155776 | tf_op jit(solution)/shard_map/reduce_scatter | solution.py:190
  1393.7 190.8 %collective-permute-start.24 = (bf16[8,1536,512]{2,1,0:T(8,128)(2,1)}, bf16[8,1536,512]{2,1,0:T(8,128)(2,1)}, u32[]{:S(2)}, u32[]{:S(2)}) collective-permute-start(bf16[8,1536,512]{2,1,0:T(8,128)(2,1)} %get-tuple-element.724.wu_ref), channel_id=1, source_target_pairs={{4,0}} | collective-permute-start | bytes 37748744 | tf_op jit(solution)/shard_map/cond/branch_0_fun/ppermute | solution.py:176
  1593.2 1.3 copy-start.3
  1593.2 1.9 copy-start.13
  1593.3 3.1 copy-start.12
  (6 other events, 4.1 us)
Sparse Core Ops, SparseCore 0:
  10.4 20.3 all-gather.26
  32.6 39.5 all-gather.22
  74.6 39.5 all-gather.10
  115.8 39.5 all-gather.18
  157.6 48.2 all-gather.14
  209.7 105.6 reduce-scatter.20
  319.5 162.9 reduce-scatter.8
  486.5 195.8 reduce-scatter.16
  686.3 169.0 reduce-scatter.12
  857.1 39.5 all-gather.24
  898.5 39.5 all-gather.12
  940.3 39.5 all-gather.20
  981.7 48.2 all-gather.16
  1033.2 105.6 reduce-scatter.22
  1202.6 105.5 reduce-scatter.10
  1393.7 105.5 reduce-scatter.18
  1593.4 81.1 reduce-scatter.14
